TPU v7x, 256 devices: a whole 4x4x8 slice. The times are simulated.
256 devices in a mesh: grp: 8 (over y, core), shard: 32 (over x, z).
Axes of the slice: x: 4, y: 4, z: 8, core: 2. Of those that a mesh axis runs over, the one named last changes fastest.
Arguments:
- grads: float32 [8, 32, 3456, 512], P('grp', 'shard'), may hold values from -6 to 6
- master: float32 [3456, 512], P('shard'), may hold values from -0.109375 to 0.109375
- moment_one: float32 [3456, 512], P('shard'), may hold values from -0.0004510549 to 0.0004510549
- moment_two: float32 [3456, 512], P('shard'), may hold values from 1.13028066e-10 to 2.8257017e-09
- step_count: int32 [1], replicated, may hold values from 1 to 59
Outputs:
- new_master: float32 [3456, 512], P('shard')
- new_moment_one: float32 [3456, 512], P('shard')
- new_moment_two: float32 [3456, 512], P('shard')
- weights: bfloat16 [3456, 512], replicated
All inputs are finite; a program needn't handle non-finite values.
Results may differ from a plain program's by a relative error of at most 0.0004.
Values may be sent and summed in bfloat16 or wider, within the bound.
A program may use at most 128 MiB of HBM per device.

v0:
```python
import jax
import jax.numpy as jnp
from jax import lax
from jax.sharding import Mesh
from jax.sharding import PartitionSpec as P

SHARD = ("shard_0", "shard_1")


def sum_by_axis(value, axes, dim):
    for axis in axes:
        value = lax.psum_scatter(value, axis, scatter_dimension=dim, tiled=True)
    return value


def sent_to_all(value, axis):
    copies = jnp.broadcast_to(value, (lax.axis_size(axis), *value.shape))
    return lax.all_to_all(copies, axis, split_axis=0, concat_axis=0, tiled=True)


def of_everyone(value, axis):
    return sent_to_all(value, axis).sum(axis=0)


def in_order(blocks, dim):
    blocks = jnp.moveaxis(blocks, 0, dim)
    lengths = blocks.shape
    return blocks.reshape(*lengths[:dim], lengths[dim] * lengths[dim + 1], *lengths[dim + 2 :])


def gather_in_order(value, axes, turns):
    blocks = value
    for k in turns:
        blocks = lax.all_gather(blocks, axes[k])
    done = turns[::-1]
    back = [done.index(k) for k in range(len(axes))]
    blocks = blocks.transpose(*back, *range(len(axes), blocks.ndim))
    return blocks.reshape(-1, *value.shape)


def gathered_by_axis(value, axes, turns, dim):
    return in_order(gather_in_order(value, axes, turns), dim)


def shards(grads, master, moment_one, moment_two, step_count):
    local = grads[0, 0]
    partial_rows = sum_by_axis(local, SHARD, 0)
    gradient = of_everyone(partial_rows, "grp")
    squares = of_everyone(jnp.sum(gradient * gradient), SHARD)
    norm = jnp.sqrt(squares)
    clip = jnp.minimum(jnp.float32(1.0), 1.0 / (norm + 1e-06))
    gradient = clip * gradient
    new_one = 0.9 * moment_one + 0.1 * gradient
    new_two = 0.999 * moment_two + 0.001 * gradient * gradient
    steps = step_count[0].astype(jnp.float32)
    first_fix = 1.0 - jnp.power(jnp.float32(0.9), steps)
    second_fix = 1.0 - jnp.power(jnp.float32(0.999), steps)
    update = new_one / first_fix / (jnp.sqrt(new_two / second_fix) + 1e-08)
    new_master = master - 0.01 * (update + 0.01 * master)
    weights = gathered_by_axis(new_master.astype(jnp.bfloat16), SHARD, (0, 1), 0)
    return (new_master, new_one, new_two, weights)


def solution(mesh):
    finer = Mesh(mesh.devices.reshape(mesh.shape["grp"], 4, 8), ("grp", "shard_0", "shard_1"))
    in_specs = (P("grp", SHARD, None, None), P(SHARD, None), P(SHARD, None), P(SHARD, None), P())
    out_specs = (P(SHARD, None), P(SHARD, None), P(SHARD, None), P())
    return jax.shard_map(
        shards, mesh=finer, in_specs=in_specs, out_specs=out_specs, check_vma=False
    )
```

profile of v0, /device:TPU:1, one launch (start us, length us, event | category | flops | bytes accessed | tf_op | source)
XLA Modules:
  0.0 246.5 jit_solution(18048320441037691581)
XLA Ops:
  7.2 0.0 reduce-scatter.4.cloned.1.call-start
  7.2 0.7 reduce-scatter.4.cloned.1.call-update
  7.9 0.0 copy-start.3
  7.9 79.3 %reduce-scatter.4.cloned.1.call-done = f32[864,512]{1,0:T(8,128)} async-done(((f32[3456,512]{1,0:T(8,128)}), f32[864,512]{1,0:T(8,128)}) %reduce-scatter.4.cloned.1.call-update) | async-done | bytes 1769488 | tf_op jit(solution)/shard_map/reduce_scatter | solution.py:12
  87.2 26.8 %fusion = f32[112,512]{1,0:T(8,128)S(1)} fusion(f32[864,512]{1,0:T(8,128)} %reduce-scatter.4.cloned.1.call-done), kind=kCustom, calls=%all-reduce-scatter | all-reduce-scatter fusion | flops 458753 | bytes 1999872
  114.1 2.5 %collective-permute-start = (f32[28,512]{1,0:T(8,128)S(1)}, f32[28,512]{1,0:T(8,128)S(1)}, u32[]{:S(2)}, u32[]{:S(2)}) collective-permute-start(f32[28,512]{1,0:T(8,128)S(1)} %slice), channel_id=1, source_target_pairs={{0,1},{1,2},{2,3},{3,4},{4,5},{5,6},{6,7},{8,9},{9,10},{10,11},{11... | collective-permute-start | bytes 172040
  116.6 0.0 copy-done.3
  116.6 0.6 dynamic-slice.4
  117.8 0.1 collective-permute-done
  117.9 0.3 concatenate
  118.2 1.5 broadcast_in_dim.6
  119.6 7.0 %all-to-all-start = ((f32[8,108,512]{2,1,0:T(8,128)}), f32[8,108,512]{2,1,0:T(8,128)S(1)}, u32[]{:S(2)}, u32[]{:S(2)}) async-start(f32[8,108,512]{2,1,0:T(8,128)} %broadcast_in_dim.6), calls=%async_computation.1 | async-start | bytes 3670016 | tf_op jit(solution)/shard_map/all_to_all | solution.py:18
  126.7 0.0 copy-start
  126.7 0.0 copy-start.1
  126.7 0.0 copy-start.2
  127.4 22.6 %all-to-all-done = f32[8,108,512]{2,1,0:T(8,128)S(1)} async-done(((f32[8,108,512]{2,1,0:T(8,128)}), f32[8,108,512]{2,1,0:T(8,128)S(1)}, u32[]{:S(2)}, u32[]{:S(2)}) %all-to-all-start) | async-done | bytes 1769504 | tf_op jit(solution)/shard_map/all_to_all | solution.py:18
  150.1 0.2 reduce_sum.27
  150.2 0.7 multiply_reduce_fusion
  150.9 1.3 broadcast_in_dim.7
  152.2 8.7 %all-to-all-start.1 = ((f32[32,1,1]{2,1,0:T(1,128)}), f32[32,1,1]{2,1,0:T(1,128)S(1)}, u32[]{:S(2)}, u32[]{:S(2)}) async-start(f32[32,1,1]{2,1,0:T(1,128)} %broadcast_in_dim.7), calls=%async_computation.2 | async-start | bytes 32768 | tf_op jit(solution)/shard_map/all_to_all | solution.py:18
  160.9 0.0 all-gather.5.cloned.1.call-start
  161.0 8.5 %all-to-all-done.1 = f32[32,1,1]{2,1,0:T(1,128)S(1)} async-done(((f32[32,1,1]{2,1,0:T(1,128)}), f32[32,1,1]{2,1,0:T(1,128)S(1)}, u32[]{:S(2)}, u32[]{:S(2)}) %all-to-all-start.1) | async-done | bytes 160 | tf_op jit(solution)/shard_map/all_to_all | solution.py:18
  169.5 0.6 reduce_sum.29
  170.9 0.0 copy-done
  170.9 0.0 copy-done.1
  170.9 0.0 copy-done.2
  170.9 1.0 convert_bitcast_fusion
  171.8 11.8 %all-gather.2 = bf16[4,108,512]{2,1,0:T(8,128)(2,1)} all-gather(bf16[1,108,512]{2,1,0:T(8,128)(2,1)S(1)} %get-tuple-element.4), channel_id=2, replica_groups=mesh['grp'=8,'shard_0'=4,'shard_1'=8] {'shard_0'}, dimensions={0}, use_global_device_ids=true | all-gather | bytes 552960 | tf_op jit(solution)/shard_map/all_gather | solution.py:34
  183.6 0.0 all-gather.5.cloned.1.call-update
  183.7 46.3 %all-gather.5.cloned.1.call-done = bf16[32,108,512]{2,1,0:T(8,128)(2,1)} async-done(((bf16[4,108,512]{2,1,0:T(8,128)(2,1)}), bf16[32,108,512]{2,1,0:T(8,128)(2,1)}) %all-gather.5.cloned.1.call-update) | async-done | bytes 3538960 | tf_op jit(solution)/shard_map/all_gather | solution.py:34
  229.9 4.2 %copy.19 = bf16[8,4,108,512]{3,2,0,1:T(8,128)(2,1)} copy(bf16[8,4,108,512]{3,2,1,0:T(8,128)(2,1)} %bitcast.14) | data formatting | bytes 7077888 | tf_op jit(solution)/shard_map/all_gather | solution.py:34
  234.1 5.6 %reshape_reshape.3 = bf16[3456,512]{1,0:T(8,128)(2,1)} reshape(bf16[4,8,108,512]{3,2,1,0:T(8,128)(2,1)} %bitcast.12) | data formatting | bytes 7077888 | tf_op jit(solution)/shard_map/reshape;reshape | solution.py:28
  (2 shorter events, 0.0 us)
Async XLA Ops:
  7.2 80.0 %reduce-scatter.4.cloned.1.call-start = ((), (), s32[]{:S(2)}) async-start(), calls=%async_computation.3 | async-start | bytes 8847360 | tf_op jit(solution)/shard_map/reduce_scatter | solution.py:12
  7.9 108.7 %copy-start.3 = (u32[256]{0:T(256)S(1)}, u32[256]{0:T(256)}, u32[]{:S(2)}) copy-start(u32[256]{0:T(256)} %constant.33) | copy-start | bytes 3076
  114.1 3.8 %collective-permute-start = (f32[28,512]{1,0:T(8,128)S(1)}, f32[28,512]{1,0:T(8,128)S(1)}, u32[]{:S(2)}, u32[]{:S(2)}) collective-permute-start(f32[28,512]{1,0:T(8,128)S(1)} %slice), channel_id=1, source_target_pairs={{0,1},{1,2},{2,3},{3,4},{4,5},{5,6},{6,7},{8,9},{9,10},{10,11},{11... | collective-permute-start | bytes 172040
  119.6 30.4 %all-to-all-start = ((f32[8,108,512]{2,1,0:T(8,128)}), f32[8,108,512]{2,1,0:T(8,128)S(1)}, u32[]{:S(2)}, u32[]{:S(2)}) async-start(f32[8,108,512]{2,1,0:T(8,128)} %broadcast_in_dim.6), calls=%async_computation.1 | async-start | bytes 3670016 | tf_op jit(solution)/shard_map/all_to_all | solution.py:18
  126.7 44.2 %copy-start = (f32[108,512]{1,0:T(8,128)S(1)}, f32[108,512]{1,0:T(8,128)}, u32[]{:S(2)}) copy-start(f32[108,512]{1,0:T(8,128)} %param.6) | copy-start | bytes 663556
  126.7 44.2 %copy-start.1 = (f32[108,512]{1,0:T(8,128)S(1)}, f32[108,512]{1,0:T(8,128)}, u32[]{:S(2)}) copy-start(f32[108,512]{1,0:T(8,128)} %param.8) | copy-start | bytes 663556
  126.7 44.2 %copy-start.2 = (f32[108,512]{1,0:T(8,128)S(1)}, f32[108,512]{1,0:T(8,128)}, u32[]{:S(2)}) copy-start(f32[108,512]{1,0:T(8,128)} %param.7) | copy-start | bytes 663556
  152.2 17.3 %all-to-all-start.1 = ((f32[32,1,1]{2,1,0:T(1,128)}), f32[32,1,1]{2,1,0:T(1,128)S(1)}, u32[]{:S(2)}, u32[]{:S(2)}) async-start(f32[32,1,1]{2,1,0:T(1,128)} %broadcast_in_dim.7), calls=%async_computation.2 | async-start | bytes 32768 | tf_op jit(solution)/shard_map/all_to_all | solution.py:18
  160.9 69.0 %all-gather.5.cloned.1.call-start = ((), (), s32[]{:S(2)}) async-start(), calls=%async_computation.4 | async-start | bytes 4128768 | tf_op jit(solution)/shard_map/all_gather | solution.py:34
Sparse Core Ops, SparseCore 0:
  10.5 76.6 reduce-scatter.3
  183.8 46.0 all-gather.4
where the time goes:
time: 247 us
  waiting for transfers between devices  157 us (64%)
  blocking collectives  38.6 us (16%)
  starting transfers between devices  18.3 us (7%)
  between operations  16.3 us (7%)
  local copies, waits for them, and re-layouts  13.4 us (5%)
    reduce_scatter x1, waiting for transfers between devices, sum_by_axis(): value = lax.psum_scatter(value, axis, scatter_dimension=dim, tiled=True)  79.3 us
    all_gather x1, waiting for transfers between devices, gather_in_order(): blocks = lax.all_gather(blocks, axes[k])  46.3 us
    all_to_all x2, waiting for transfers between devices, sent_to_all(): return lax.all_to_all(copies, axis, split_axis=0, concat_axis=0, tiled=True)  31.1 us
    unnamed x1, blocking collectives  26.8 us
    all_to_all x2, starting transfers between devices, sent_to_all(): return lax.all_to_all(copies, axis, split_axis=0, concat_axis=0, tiled=True)  15.8 us
    all_gather x1, blocking collectives, gather_in_order(): blocks = lax.all_gather(blocks, axes[k])  11.8 us
    another operation x1, local copies, waits for them, and re-layouts, in_order(): blocks.reshape(*lengths[:dim], lengths[dim] * lengths[dim + 1], *lengths[...  5.56 us
  transfers between devices with their start and end apart: 5, of which 5 were waited for; matrix products, arithmetic and copies ran while one was open for 0% of the time, Pallas kernels for 0%

commit v1 on v0

v1 whole, which is shorter than its diff:
```python
import functools

import jax
import jax.numpy as jnp
from jax import lax
from jax.experimental import pallas as pl
from jax.experimental.pallas import tpu as pltpu
from jax.sharding import PartitionSpec as P

MESH = pl.DeviceIdType.MESH
ROWS = 108
WIN = 112
LANES = 128
FAR, PLAIN, ACC = 0, 1, 2


def coded(value):
    top = jnp.maximum(jnp.max(jnp.abs(value), axis=0, keepdims=True), 1e-30)
    steps = jnp.round(value * (32767.0 / top))
    return steps.astype(jnp.int32).astype(jnp.int16), top * (1.0 / 32767.0)


def decoded(steps, scale):
    return steps.astype(jnp.int32).astype(jnp.float32) * scale


def kernel(
    grads, master_, one_, two_, fixes,
    new_master, new_one, new_two, weights,
    master, one, two, state_sem, own_a, own_b, sib_a, sib_b,
    tx1, ts1, rx1, rs1, tx2, ts2, rx2, rs2, first, second,
    ztx, zts, zrx, zrs, total, plane, line, sum_of, wide, gathered,
    own_sem, d2d_s, d2d_r, s1, r1, ss1, sr1, s2, r2, ss2, sr2,
    zs, zr, zss, zsr, gs, gr, ps, pr, ls, lr, os, or_, ws, wr, as1, ar1, as2, ar2, fs, fr,
):
    g = lax.axis_index("grp")
    s = lax.axis_index("shard")
    y, c = g // 2, g % 2
    x, z = s // 8, s % 8
    odd = z % 2
    part = z // 4

    def core_of(z_):
        return (z_ // 2) % 2

    owner = c == core_of(z)

    def dev(x_=x, y_=y, z_=z, c_=c):
        return (y_ * 2 + c_, x_ * 8 + z_)

    def remote(src, dst, send, recv, device):
        return pltpu.make_async_remote_copy(
            src_ref=src, dst_ref=dst, send_sem=send, recv_sem=recv, device_id=device, device_id_type=MESH
        )

    def ring(a, n, k):
        return (a + k) % n

    sends = []

    def go(copy):
        copy.start()
        sends.append(copy)

    def lanes(t):
        return pl.ds(pl.multiple_of(LANES * ring(y, 4, t), LANES), LANES)

    def chunk(p, j, core):
        if p == 0:
            return grads.at[ring(x, 4, j), pl.ds(pl.multiple_of(216 * core, 8), 216)]
        return grads.at[:, pl.ds(pl.multiple_of(432 + 216 * core, 8), 216), lanes(j)]

    own, sib = (own_a, own_b), (sib_a, sib_b)
    order = [(0, 2), (1, 2), (0, 1), (0, 3), (1, 1), (1, 3), (0, 0), (1, 0)]
    loads = {}
    for n, (p, j) in enumerate(order):
        loads[p, j] = pltpu.make_async_copy(chunk(p, j, c), own[p].at[j], own_sem.at[n])
        loads[p, j].start()
    state = [
        pltpu.make_async_copy(src, dst, state_sem.at[n])
        for n, (src, dst) in enumerate(((master_, master), (one_, one), (two_, two)))
    ]
    for copy in state:
        copy.start()

    plane_of = [(i, k) for i in range(4) for k in range(4) if i or k]
    barrier = pltpu.get_barrier_semaphore()
    partners = [dev(c_=1 - c)]
    partners += [dev(x_=ring(x, 4, i), y_=ring(y, 4, k)) for i, k in plane_of]
    partners += [dev(z_=ring(z, 8, k), c_=core) for k in range(1, 8) for core in (c, 1 - c)]
    for partner in partners:
        pl.semaphore_signal(barrier, inc=1, device_id=partner, device_id_type=MESH)
    pl.semaphore_wait(barrier, len(partners))

    pairs = {}
    for n, (p, j) in enumerate(order):
        pairs[p, j] = remote(chunk(p, j, 1 - c), sib[p].at[j], d2d_s.at[n], d2d_r.at[n], dev(c_=1 - c))
        go(pairs[p, j])

    def chip_ready(p, j):
        loads[p, j].wait()
        pairs[p, j].wait_recv()

    def chip_a(j, e, i):
        at = (j, pl.ds(104 * e, WIN), lanes(i))
        return own_a[at] + sib_a[at]

    def chip_b(j, e, i):
        at = (j, ring(x, 4, i), pl.ds(104 * e, WIN))
        return own_b[at] + sib_b[at]

    along_x = [dev(x_=ring(x, 4, 1)), dev(x_=ring(x, 4, 3))]
    along_y = [dev(y_=ring(y, 4, 1)), dev(y_=ring(y, 4, 3))]

    class Scatter:
        def __init__(self, value, many, ends, base, bufs, sems):
            self.value, self.many, self.ends, self.base = value, many, ends, base
            self.tx, self.ts, self.rx, self.rs = bufs
            self.sems = sems

        def slot(self, d, kind, i):
            return (self.base * 6 + d * 3 + kind) * self.many + i

        def copies(self, d, kind, i):
            n = self.slot(d, kind, i)
            send, recv, scale_send, scale_recv = self.sems
            return (
                remote(self.tx.at[n], self.rx.at[n], send.at[n], recv.at[n], self.ends[d]),
                remote(self.ts.at[n], self.rs.at[n], scale_send.at[n], scale_recv.at[n], self.ends[d]),
            )

        def arrived(self, d, kind, i):
            n = self.slot(d, kind, i)
            for copy in self.copies(d, kind, i):
                copy.wait_recv()
            return decoded(self.rx[n], self.rs[n])

        def send(self, d, kind, i):
            n = self.slot(d, kind, i)
            j = 2 if kind == FAR else (1, 3)[d]
            half = 1 - d if kind == PLAIN else d
            value = self.value(j, half, i)
            if kind == ACC:
                value = value + self.arrived(d, FAR, i)
            self.tx[n], self.ts[n] = coded(value)
            for copy in self.copies(d, kind, i):
                go(copy)

        def result(self, e, i):
            return self.value(0, e, i) + self.arrived(1 - e, PLAIN, i) + self.arrived(e, ACC, i)

    bufs1, sems1 = (tx1, ts1, rx1, rs1), (s1, r1, ss1, sr1)
    bufs2, sems2 = (tx2, ts2, rx2, rs2), (s2, r2, ss2, sr2)
    sc = [Scatter(chip_a, 4, along_x, 0, bufs1, sems1), Scatter(chip_b, 4, along_y, 1, bufs1, sems1)]
    nxt = [
        Scatter(lambda j, e, i: first[0, e, j], 1, along_y, 0, bufs2, sems2),
        Scatter(lambda j, e, i: first[1, e, j], 1, along_x, 1, bufs2, sems2),
    ]
    turns = (2, 1, 3, 0)

    for p in (0, 1):
        chip_ready(p, 2)
        for i in turns:
            for d in (0, 1):
                sc[p].send(d, FAR, i)
    for p in (0, 1):
        chip_ready(p, 1)
        chip_ready(p, 3)
        for d in (0, 1):
            sc[p].send(d, PLAIN, 2)
    for i in turns:
        for p in (0, 1):
            for d in (0, 1):
                if i != 2:
                    sc[p].send(d, PLAIN, i)
                sc[p].send(d, ACC, i)
    for p in (0, 1):
        chip_ready(p, 0)

    for i in turns:
        for p in (0, 1):
            for e in (0, 1):
                first[p, e, i] = sc[p].result(e, i)
            if i == 2:
                for d in (0, 1):
                    nxt[p].send(d, FAR, 0)
            elif i:
                nxt[p].send((i - 1) // 2, PLAIN, 0)
    for p in (0, 1):
        for d in (0, 1):
            nxt[p].send(d, ACC, 0)

    def z_copies(n, there, slot):
        device = dev(z_=there)
        return (
            remote(ztx.at[n], zrx.at[slot], zs.at[n], zr.at[slot], device),
            remote(zts.at[n], zrs.at[slot], zss.at[n], zsr.at[slot], device),
        )

    for p in (0, 1):
        for e in (0, 1):
            n = 2 * p + e
            there = 4 * p + 2 * c + e
            value = nxt[p].result(e, 0)
            second[n] = value
            ztx[n], zts[n] = coded(value)

            @pl.when(there != z)
            def _():
                for copy in z_copies(n, there, (z - there + 8) % 8):
                    copy.start()

    row = lax.broadcasted_iota(jnp.int32, (WIN, LANES), 0)

    def plane_copy(i, k):
        back = 4 * ((4 - i) % 4) + (4 - k) % 4
        return remote(plane.at[0], plane.at[back], ps.at[4 * i + k], pr.at[back], dev(x_=ring(x, 4, i), y_=ring(y, 4, k)))

    def line_copy(k):
        there = ring(z, 8, k)
        return remote(line.at[0], line.at[8 - k], ls.at[k], lr.at[8 - k], dev(z_=there, c_=core_of(there)))

    def sum_copy():
        return remote(sum_of, sum_of, os.at[0], or_.at[0], dev(c_=1 - c))

    def total_copy(k):
        return remote(total.at[0], total.at[(4 - k) % 4], gs.at[k], gr.at[(4 - k) % 4], dev(y_=ring(y, 4, k)))

    def total_across(k):
        return remote(total.at[k], total.at[k], gs.at[4 + k], gr.at[4 + k], dev(c_=1 - c))

    def i_own(p):
        return x + p * (y - x)

    def j_own(p):
        return y + p * (x - y)

    def weight_copy(n, there, p, e):
        at = gathered.at[c, p, i_own(p), e, j_own(p)]
        return remote(at, at, ws.at[n], wr.at[2 * p + e], dev(z_=there))

    first_fix, second_fix = fixes[0], fixes[1]
    for copy in state:
        copy.wait()

    def update(summed, at):
        squares = jnp.sum(sum_of[...], axis=1, keepdims=True)
        clip = jnp.minimum(1.0, 1.0 / (jnp.sqrt(squares) + 1e-06))
        gradient = clip * summed
        first_moment = 0.9 * one[:, at] + 0.1 * gradient
        second_moment = 0.999 * two[:, at] + 0.001 * gradient * gradient
        step = first_moment / first_fix / (jnp.sqrt(second_moment / second_fix) + 1e-08)
        return master[:, at] - 0.01 * (step + 0.01 * master[:, at]), first_moment, second_moment

    @pl.when(owner)
    def _():
        value = second[2 * part + odd]
        for k in range(1, 8):
            for copy in z_copies(0, z, k):
                copy.wait_recv()
            value = value + decoded(zrx[k], zrs[k])
        value = jnp.where(odd == 1, pltpu.roll(value, WIN - 4, 0), value)
        value = jnp.where(row < ROWS, value, 0.0)
        total[0] = value
        plane[0] = jnp.sum(value * value, axis=0, keepdims=True)
        for i, k in plane_of:
            plane_copy(i, k).start()
        for i, k in plane_of:
            plane_copy(i, k).wait_recv()
        value = jnp.zeros((1, LANES), jnp.float32)
        for i in range(4):
            for k in range(4):
                value = value + plane[4 * ring(i, 4, 4 - x) + ring(k, 4, 4 - y)]
        line[0] = value
        for k in range(1, 8):
            line_copy(k).start()
        for k in range(1, 8):
            line_copy(k).wait_recv()
        value = line[(8 - z) % 8]
        for k in range(1, 8):
            value = value + line[(k + 8 - z) % 8]
        sum_of[...] = value
        wide[...] = jnp.zeros_like(wide)
        wide[0:ROWS] = update(total[0, 0:ROWS], lanes(0))[0]
        value = wide[...]
        value = jnp.where(odd == 1, pltpu.roll(value, 4, 0), value)
        gathered[c, part, i_own(part), odd, j_own(part)] = value.astype(jnp.bfloat16)
        for k in (4, 3, 5, 2, 6, 1, 7):
            weight_copy(k, ring(z, 8, k), part, odd).start()
        sum_copy().start()
        for k in (1, 2, 3):
            total_copy(k).start()

    class Gather:
        def __init__(self, slot, here, ends, base, sems, many=1):
            self.slot, self.here, self.ends, self.base, self.sems = slot, here, ends, base, sems
            self.many = many

        def copy(self, d, kind, half, k, j=0):
            n = (self.base * 6 + d * 3 + kind) * self.many + j
            at = self.slot(half, ring(self.here, 4, k), j)
            return remote(at, at, self.sems[0].at[n], self.sems[1].at[n], self.ends[d])

        def start(self, half, j=0):
            for d in (half, 1 - half):
                go(self.copy(d, 0 if half == d else 1, half, 0, j))

        def pass_on(self, d, j=0):
            back = (3, 1)[d]
            self.copy(d, 0, d, back, j).wait_recv()
            go(self.copy(d, 2, d, back, j))

        def near(self, d, j=0):
            self.copy(d, 1, 1 - d, (3, 1)[d], j).wait_recv()

        def far(self, d, j=0):
            self.copy(d, 2, d, 2, j).wait_recv()

    near = [
        Gather(lambda e, k, j: gathered.at[c, 0, x, e, k], y, along_y, 0, (as1, ar1)),
        Gather(lambda e, k, j: gathered.at[c, 1, y, e, k], x, along_x, 1, (as1, ar1)),
    ]
    wider = [
        Gather(lambda e, k, j: gathered.at[c, 0, k, e, ring(y, 4, j)], x, along_x, 0, (as2, ar2), 4),
        Gather(lambda e, k, j: gathered.at[c, 1, k, e, ring(x, 4, j)], y, along_y, 1, (as2, ar2), 4),
    ]

    def across(p, k, e):
        at = gathered.at[c, p, ring((x, y)[p], 4, k), e]
        n = 8 * p + 2 * k + e
        return remote(at, at, fs.at[n], fr.at[n], dev(c_=1 - c))

    def place(p, k, t):
        i = ring((x, y)[p], 4, k)
        pieces = []
        for core in (0, 1):
            low = gathered[core, p, i, 0, t].astype(jnp.float32)
            high = gathered[core, p, i, 1, t].astype(jnp.float32)
            mixed = jnp.where(row[0:8] < 4, low[104:112], high[0:8])
            pieces += [low[0:104], mixed, high[8:112]]
        value = jnp.concatenate(pieces, axis=0).astype(jnp.bfloat16)
        block, column = (i, t) if p == 0 else (t, i)
        weights[
            pl.ds(pl.multiple_of(864 * block + 432 * p, 16), 432),
            pl.ds(pl.multiple_of(LANES * column, LANES), LANES),
        ] = value

    def place_all(p, k):
        for e in (0, 1):
            across(p, k, e).wait_recv()
        lax.fori_loop(0, 4, lambda t, _: (place(p, k, t), 0)[1], 0)

    both = [(p, e) for p in (0, 1) for e in (0, 1)]
    for p, e in both:
        there = 4 * p + 2 * c + e

        @pl.when(there != z)
        def _():
            weight_copy(0, z, p, e).wait_recv()

        near[p].start(e)
    for p, e in both:
        wider[p].start(e, 0)
    for p, d in both:
        near[p].pass_on(d)
        wider[p].start(d, (3, 1)[d])
    for p, d in both:
        near[p].near(d)
        wider[p].start(1 - d, (3, 1)[d])
    for p, d in both:
        wider[p].pass_on(d, 0)
    for p, d in both:
        near[p].far(d)
        wider[p].start(d, 2)
    for p, e in both:
        go(across(p, 0, e))

    @pl.when(owner)
    def _():
        for k in (1, 2, 3):
            total_copy(4 - k).wait_recv()
        for k in range(4):
            total_across(k).start()

    @pl.when(jnp.logical_not(owner))
    def _():
        sum_copy().wait_recv()
        for k in range(4):
            total_across(k).wait_recv()

    for k in range(4):
        at = lanes(k)
        new_master[:, at], new_one[:, at], new_two[:, at] = update(total[k, 0:ROWS], at)

    for j in (3, 1):
        for p, d in both:
            wider[p].pass_on(d, j)
    for p in (0, 1):
        place_all(p, 0)
    for p, d in both:
        wider[p].pass_on(d, 2)
        go(across(p, (3, 1)[d], d))
    for p, d in both:
        for j in (0, 3, 1, 2):
            wider[p].near(d, j)
        go(across(p, (3, 1)[d], 1 - d))
    for p, d in both:
        for j in (0, 3, 1, 2):
            wider[p].far(d, j)
        go(across(p, 2, d))
    for k in (1, 3, 2):
        for p in (0, 1):
            place_all(p, k)

    for copy in sends:
        copy.wait_send()
    for p, e in both:
        there = 4 * p + 2 * c + e

        @pl.when(there != z)
        def _():
            for copy in z_copies(2 * p + e, there, (z - there + 8) % 8):
                copy.wait_send()

    @pl.when(owner)
    def _():
        for i, k in plane_of:
            plane_copy(i, k).wait_send()
        for k in range(1, 8):
            line_copy(k).wait_send()
            weight_copy(k, ring(z, 8, k), part, odd).wait_send()
        sum_copy().wait_send()
        for k in (1, 2, 3):
            total_copy(k).wait_send()
        for k in range(4):
            total_across(k).wait_send()


def finish(*refs):
    sources, results, sems = refs[:4], refs[4:8], refs[8]
    copies = [pltpu.make_async_copy(src, dst, sems.at[n]) for n, (src, dst) in enumerate(zip(sources, results))]
    for copy in copies[::-1]:
        copy.start()
    for copy in copies:
        copy.wait()


def shards(grads, master, moment_one, moment_two, step_count):
    steps = step_count[0].astype(jnp.float32)
    fixes = jnp.stack([1.0 - jnp.power(jnp.float32(0.9), steps), 1.0 - jnp.power(jnp.float32(0.999), steps)])
    vmem = pl.BlockSpec(memory_space=pltpu.VMEM)
    f32, i16, bf16 = jnp.float32, jnp.int16, jnp.bfloat16
    dma = pltpu.SemaphoreType.DMA
    state = jax.ShapeDtypeStruct((ROWS, 512), f32)
    results = (state, state, state, jax.ShapeDtypeStruct((3456, 512), bf16))
    hbm, anywhere = pl.BlockSpec(memory_space=pltpu.HBM), pl.BlockSpec(memory_space=pl.ANY)
    grads = grads.reshape(4, 864, 512)
    grads, master, moment_one, moment_two = (
        pltpu.with_memory_space_constraint(value, pltpu.HBM) for value in (grads, master, moment_one, moment_two)
    )
    made = pl.pallas_call(
        kernel,
        out_shape=results,
        in_specs=[hbm, hbm, hbm, hbm, pl.BlockSpec(memory_space=pltpu.SMEM)],
        out_specs=(vmem, vmem, vmem, vmem),
        scratch_shapes=[
            pltpu.VMEM((ROWS, 512), f32),
            pltpu.VMEM((ROWS, 512), f32),
            pltpu.VMEM((ROWS, 512), f32),
            dma((3,)),
            pltpu.VMEM((4, 216, 512), f32),
            pltpu.VMEM((4, 4, 216, LANES), f32),
            pltpu.VMEM((4, 216, 512), f32),
            pltpu.VMEM((4, 4, 216, LANES), f32),
            pltpu.VMEM((48, WIN, LANES), i16),
            pltpu.VMEM((48, 1, LANES), f32),
            pltpu.VMEM((48, WIN, LANES), i16),
            pltpu.VMEM((48, 1, LANES), f32),
            pltpu.VMEM((12, WIN, LANES), i16),
            pltpu.VMEM((12, 1, LANES), f32),
            pltpu.VMEM((12, WIN, LANES), i16),
            pltpu.VMEM((12, 1, LANES), f32),
            pltpu.VMEM((2, 2, 4, WIN, LANES), f32),
            pltpu.VMEM((4, WIN, LANES), f32),
            pltpu.VMEM((4, WIN, LANES), i16),
            pltpu.VMEM((4, 1, LANES), f32),
            pltpu.VMEM((8, WIN, LANES), i16),
            pltpu.VMEM((8, 1, LANES), f32),
            pltpu.VMEM((4, WIN, LANES), f32),
            pltpu.VMEM((16, 1, LANES), f32),
            pltpu.VMEM((8, 1, LANES), f32),
            pltpu.VMEM((1, LANES), f32),
            pltpu.VMEM((WIN, LANES), f32),
            pltpu.VMEM((2, 2, 4, 2, 4, WIN, LANES), bf16),
            dma((8,)), dma((8,)), dma((8,)),
            dma((48,)), dma((48,)), dma((48,)), dma((48,)),
            dma((12,)), dma((12,)), dma((12,)), dma((12,)),
            dma((4,)), dma((8,)), dma((4,)), dma((8,)),
            dma((8,)), dma((8,)),
            dma((16,)), dma((16,)), dma((8,)), dma((8,)), dma((1,)), dma((1,)),
            dma((8,)), dma((4,)),
            dma((12,)), dma((12,)), dma((48,)), dma((48,)),
            dma((16,)), dma((16,)),
        ],
        compiler_params=pltpu.CompilerParams(collective_id=0, has_side_effects=True, vmem_limit_bytes=24 * 2**20),
        name="step",
    )(grads, master, moment_one, moment_two, fixes)
    return pl.pallas_call(
        finish,
        out_shape=results,
        in_specs=[anywhere] * 4,
        out_specs=(hbm, hbm, hbm, hbm),
        scratch_shapes=[dma((4,))],
        compiler_params=pltpu.CompilerParams(vmem_limit_bytes=2**20),
        name="finish",
    )(*made)


def solution(mesh):
    in_specs = (P("grp", "shard", None, None), P("shard", None), P("shard", None), P("shard", None), P())
    out_specs = (P("shard", None), P("shard", None), P("shard", None), P())
    return jax.shard_map(shards, mesh=mesh, in_specs=in_specs, out_specs=out_specs, check_vma=False)
```

time: 247 us -> 71.9 us (0.29)
  waiting for transfers between devices: 157 us -> 0 us
  Pallas kernels: 0 us -> 70.4 us
  blocking collectives: 38.6 us -> 0 us
  starting transfers between devices: 18.3 us -> 0 us
  between operations: 16.3 us -> 1.37 us
  local copies, waits for them, and re-layouts: 13.4 us -> 0 us
    reduce_scatter x1 -> x0, waiting for transfers between devices: 79.3 us -> none  [sum_by_axis(): value = lax.psum_scatter(value, axis, scatter_dimension=dim, tiled=True)]
    pallas_call x0 -> x2, Pallas kernels: none -> 70.4 us  [the longest x1 68.4 us: shards(): pl.pallas_call(kernel, out_shape=results, in_specs=[hbm, hbm, hbm, hbm, p...]
    all_gather x1 -> x0, waiting for transfers between devices: 46.3 us -> none  [gather_in_order(): blocks = lax.all_gather(blocks, axes[k])]
    all_to_all x2 -> x0, waiting for transfers between devices: 31.1 us -> none  [sent_to_all(): return lax.all_to_all(copies, axis, split_axis=0, concat_axis=0, tiled=True)]
    unnamed x1 -> x0, blocking collectives: 26.8 us -> none
    all_to_all x2 -> x0, starting transfers between devices: 15.8 us -> none  [sent_to_all(): return lax.all_to_all(copies, axis, split_axis=0, concat_axis=0, tiled=True)]
    all_gather x1 -> x0, blocking collectives: 11.8 us -> none  [gather_in_order(): blocks = lax.all_gather(blocks, axes[k])]
    another operation x1 -> x0, local copies, waits for them, and re-layouts: 5.56 us -> none  [in_order(): blocks.reshape(*lengths[:dim], lengths[dim] * lengths[dim + 1], *lengths[...]
  transfers between devices with their start and end apart: 5 -> 0, of which waited for: 5 -> 0; matrix products, arithmetic and copies ran while one was open for 0% -> 0% of each run, Pallas kernels for 0% -> 0%
where the time goes in v1:
time: 71.9 us; the launch traced here: 71.8 us
  Pallas kernels  70.4 us (98%)
  between operations  1.37 us (2%)
    pallas_call x1, Pallas kernels, shards(): pl.pallas_call(kernel, out_shape=results, in_specs=[hbm, hbm, hbm, hbm, p...  68.4 us
    pallas_call x1, Pallas kernels, shards(): pl.pallas_call(finish, out_shape=results, in_specs=[anywhere] * 4, out_sp...  2.04 us

profile of v1, /device:TPU:1, one launch (start us, length us, event | category | flops | bytes accessed | tf_op | source)
XLA Modules:
  0.0 71.8 jit_solution(8236578218543217687)
XLA Ops:
  1.4 0.1 pad_maximum_fusion.fixes
  1.4 68.4 %step.1 = (f32[108,512]{1,0:T(8,128)S(1)}, f32[108,512]{1,0:T(8,128)S(1)}, f32[108,512]{1,0:T(8,128)S(1)}, bf16[3456,512]{1,0:T(8,128)(2,1)S(1)}) custom-call(f32[4,864,512]{2,1,0:T(8,128)} %bitcast.1, f32[108,512]{1,0:T(8,128)} %master_.1, f32[108,512]{1,0:T(8,128)} %one_.1, f32[108,512]{1,0:T(8,128)} %two_.1, f32[2]{0:T(128)S(1)} %pad_maximum_fusion.fixes), custom_call_target="tpu_custom_call" | custom-call | tf_op jit(solution)/shard_map/step/pallas_call | solution.py:461
  69.8 2.0 %finish.1 = (f32[108,512]{1,0:T(8,128)}, f32[108,512]{1,0:T(8,128)}, f32[108,512]{1,0:T(8,128)}, bf16[3456,512]{1,0:T(8,128)(2,1)}) custom-call(f32[108,512]{1,0:T(8,128)S(1)} %get-tuple-element.8.refs_0_, f32[108,512]{1,0:T(8,128)S(1)} %get-tuple-element.9.refs_1_, f32[108,512]{1,0:T(8,128)S(1)} %get-tuple-element.10.refs_2_, ...), custom_call_target="tpu_custom_call" | custom-call | tf_op jit(solution)/shard_map/finish/pallas_call | solution.py:508
